TPU v7x, 32 devices: a whole 2x2x4 slice. The times are simulated.
32 devices in a mesh: gz: 32 (over z, y, x, core).
Axes of the slice: x: 2, y: 2, z: 4, core: 2. Of those that a mesh axis runs over, the one named last changes fastest.
Arguments:
- right_side: float32 [64, 512, 512], P('gz'), may hold values from -20 to 20
- cell_flags: int32 [64, 512, 512], P('gz'), may hold values from 0 to 2
Outputs:
- solution: float32 [64, 512, 512], P('gz')
- residual: float32 [64, 512, 512], P('gz')
All inputs are finite; a program needn't handle non-finite values.
Results may differ from a plain program's by a relative error of at most 0.00011.
Values sent between devices are 32-bit elements; how exact they have to be, the bound alone decides.
A program may use at most 128 MiB of HBM per device.

v0:
```python
import jax
import jax.numpy as jnp
from jax import lax
from jax.sharding import PartitionSpec as P

ITERS = 2


def extended_2(cells, sides, width):
    for axis, dim in sides:
        count = lax.axis_size(axis)
        ends = count - 1
        head = lax.slice_in_dim(cells, 0, width, axis=dim)
        tail = lax.slice_in_dim(cells, cells.shape[dim] - width, cells.shape[dim], axis=dim)
        cells = jnp.concatenate(
            [
                lax.ppermute(tail, axis, [(i, (i + 1) % count) for i in range(ends)]),
                cells,
                lax.ppermute(head, axis, [((i + 1) % count, i) for i in range(ends)]),
            ],
            axis=dim,
        )
    return cells


def neighbour_total(extended):
    centre = extended[1:-1]
    inplane = jnp.pad(centre, ((0, 0), (1, 1), (1, 1)))
    total = extended[2:] + extended[:-2]
    total = total + inplane[:, 2:, 1:-1] + inplane[:, :-2, 1:-1]
    total = total + inplane[:, 1:-1, 2:] + inplane[:, 1:-1, :-2]
    return total


def apply_operator(extended, diagonal, fluid_mask):
    return fluid_mask * (diagonal * extended[1:-1] - neighbour_total(extended))


def diagonal_from_solid(solid_extended):
    return jnp.maximum(6.0 - neighbour_total(solid_extended), 1.0)


def build_diagonal(cell_flags):
    solid_bits = (cell_flags == 2).astype(jnp.int32)
    depth, rows, cols = solid_bits.shape
    shifts = jnp.arange(32, dtype=jnp.int32)
    weights = jnp.left_shift(jnp.ones((32,), jnp.int32), shifts)
    packed = jnp.sum(
        solid_bits.reshape(depth, rows // 32, 32, cols) * weights[None, None, :, None],
        axis=2,
        dtype=jnp.int32,
    )
    rims = extended_2(packed, (("gz", 0),), 1)
    edges = jnp.concatenate([rims[:1], rims[-1:]], axis=0)
    unpacked = jnp.bitwise_and(
        jnp.right_shift(edges[:, :, None, :], shifts[None, None, :, None]), 1
    )
    unpacked = unpacked.reshape(2, rows, cols).astype(jnp.float32)
    extended = jnp.concatenate([unpacked[:1], solid_bits.astype(jnp.float32), unpacked[1:]], axis=0)
    return diagonal_from_solid(extended)


def body(right_side, cell_flags):
    widest = 0
    fluid_mask = (cell_flags == 1).astype(jnp.float32)
    diagonal = build_diagonal(cell_flags)
    residual = fluid_mask * right_side

    def operate(field, margin):
        extended = extended_2(field, (("gz", 0),), 1)
        return (apply_operator(extended, diagonal, fluid_mask), margin)

    margin = widest
    solution = jnp.zeros_like(residual)
    precond = residual / diagonal
    applied, inner = operate(precond, margin)
    margin = inner
    direction = precond
    along = applied
    rz_old = None
    step_old = None
    for iteration in range(ITERS):
        rz_now, product = lax.psum((jnp.sum(residual * precond), jnp.sum(applied * precond)), "gz")
        if iteration == 0:
            step_size = rz_now / product
            direction = precond
            along = applied
        else:
            blend_factor = rz_now / rz_old
            step_size = rz_now / (product - blend_factor * rz_now / step_old)
            direction = precond + blend_factor * direction
            along = applied + blend_factor * along
        solution = solution + step_size * direction
        residual = residual - step_size * along
        rz_old = rz_now
        step_old = step_size
        if iteration + 1 < ITERS:
            precond = residual / diagonal
            applied, inner = operate(precond, margin)
            margin = inner
    return (solution, residual)


def solution(mesh):
    placed = (P("gz", None, None), P("gz", None, None))
    return jax.shard_map(
        body,
        mesh=mesh,
        in_specs=placed,
        out_specs=(P("gz", None, None), P("gz", None, None)),
        check_vma=False,
    )
```

profile of v0, /device:TPU:0, one launch (start us, length us, event | category | flops | bytes accessed | tf_op | source)
XLA Modules:
  0.0 180.5 jit_solution(2949102520636874230)
XLA Ops:
  0.6 0.0 copy-start.6
  0.7 2.2 %multiply_reduce_fusion.4 = s32[2,16,512]{2,1,0:T(8,128)S(1)} fusion(s32[32]{0:T(128)S(1)} %iota_shift-left_fusion, s32[2,512,512]{2,1,0:T(8,128)} %param.3), kind=kLoop, calls=%fused_computation.49 | loop fusion | flops 2080768 | bytes 2162816 | tf_op jit(solution)/shard_map/reduce_sum | solution.py:48
  2.9 2.4 %collective-permute-start = (s32[1,16,512]{2,1,0:T(8,128)S(1)}, s32[1,16,512]{2,1,0:T(8,128)S(1)}, u32[]{:S(2)}, u32[]{:S(2)}) collective-permute-start(s32[1,16,512]{2,1,0:T(8,128)S(1)} %get-tuple-element.21), channel_id=1, source_target_pairs={{0,1},{1,2},{2,3},{3,4},{4,5},{5,6},{6,7},{7,8},{8,9},{9,10},{10,1... | collective-permute-start | bytes 98312 | tf_op jit(solution)/shard_map/ppermute | solution.py:17
  5.3 1.3 collective-permute-start.1
  6.6 1.6 fusion.24
  8.2 0.1 shift_right_arithmetic.23
  8.2 2.2 %collective-permute-done.1 = s32[1,16,512]{2,1,0:T(8,128)S(1)} collective-permute-done((s32[1,16,512]{2,1,0:T(8,128)S(1)}, s32[1,16,512]{2,1,0:T(8,128)S(1)}, u32[]{:S(2)}, u32[]{:S(2)}) %collective-permute-start.1) | collective-permute-done | bytes 32800 | tf_op jit(solution)/shard_map/ppermute | solution.py:19
  10.5 0.3 fusion.22
  10.8 0.0 copy-start
  10.8 0.0 copy-start.7
  10.8 0.2 fusion.31
  11.0 1.1 copy-done.8
  12.1 0.7 copy-done
  12.8 0.6 copy-done.7
  13.4 2.2 %fusion.23 = (f32[2,512,512]{2,1,0:T(8,128)S(1)}, pred[2,512,512]{2,1,0:T(8,128)(4,1)S(1)}, f32[2,512,512]{2,1,0:T(8,128)S(1)}) fusion(f32[2,512,512]{2,1,0:T(8,128)S(1)} %copy-done, s32[2,512,512]{2,1,0:T(8,128)S(1)} %copy-done.7, f32[2,512,512]{2,1,0:T(8,128)S(1)} %copy-done.8, f32[1,512,512]{2,1,0:T(8,128)S(1)} %get-tuple-element.20, ...), kind=kLoop, calls=%fused_computation.52 | loop fusion | flops 6291456 | bytes 13107200 | tf_op jit(solution)/shard_map/div | solution.py:75
  15.7 0.2 fusion.30
  15.9 1.3 collective-permute-start.2
  17.2 5.2 %collective-permute-start.3 = (f32[1,512,512]{2,1,0:T(8,128)S(1)}, f32[1,512,512]{2,1,0:T(8,128)S(1)}, u32[]{:S(2)}, u32[]{:S(2)}) collective-permute-start(f32[1,512,512]{2,1,0:T(8,128)S(1)} %get-tuple-element.18), channel_id=1, source_target_pairs={{0,1},{1,2},{2,3},{3,4},{4,5},{5,6},{6,7},{7,8},{8,9},{9,10},{10,1... | collective-permute-start | bytes 3145736 | tf_op jit(solution)/shard_map/ppermute | solution.py:17
  22.4 0.1 collective-permute-done.2
  22.5 2.1 %collective-permute-done.3 = f32[1,512,512]{2,1,0:T(8,128)S(1)} collective-permute-done((f32[1,512,512]{2,1,0:T(8,128)S(1)}, f32[1,512,512]{2,1,0:T(8,128)S(1)}, u32[]{:S(2)}, u32[]{:S(2)}) %collective-permute-start.3) | collective-permute-done | bytes 1048608 | tf_op jit(solution)/shard_map/ppermute | solution.py:17
  24.6 4.2 %multiply_reduce_fusion.2 = (f32[]{:T(128)}, f32[]{:T(128)}, f32[2,512,512]{2,1,0:T(8,128)}) fusion(f32[2,512,512]{2,1,0:T(8,128)S(1)} %get-tuple-element.12, pred[2,512,512]{2,1,0:T(8,128)(4,1)S(1)} %get-tuple-element.13, f32[2,512,512]{2,1,0:T(8,128)S(1)} %copy-done, f32[1,512,512]{2,1,0:T(8,128)S(1)} %collective-permute-done.3, ...), kind=kLoop, calls=%fused_computation.47 | loop fusion | flops 7864318 | bytes 11010056 | tf_op jit(solution)/shard_map/reduce_sum | solution.py:83
  28.8 63.0 %all-reduce.4 = (f32[]{:T(128)}, f32[]{:T(128)}) all-reduce(f32[]{:T(128)} %get-tuple-element.5, f32[]{:T(128)} %get-tuple-element.4), channel_id=1, replica_groups=mesh['gz'=32] {'gz'}, use_global_device_ids=true, to_apply=%region_2.3 | all-reduce | flops 2 | bytes 16 | tf_op jit(solution)/shard_map/psum | solution.py:83
  93.1 3.1 %fusion.25 = f32[2,512,512]{2,1,0:T(8,128)S(1)} fusion(f32[2,512,512]{2,1,0:T(8,128)} %copy-done.3, f32[2,512,512]{2,1,0:T(8,128)} %get-tuple-element.11, f32[]{:T(128)S(6)} %div.19, pred[2,512,512]{2,1,0:T(8,128)(4,1)S(1)} %get-tuple-element.13, f32[2,512,512]{2,1,0:T(8,128)S(1)} %copy-done), kind=kLoop, calls=%fused_computation.57 | loop fusion | flops 2097152 | bytes 8912900 | tf_op jit(solution)/shard_map/div | solution.py:98
  96.2 0.0 copy-start.4
  96.2 0.2 fusion.29
  96.4 1.6 collective-permute-start.4
  98.0 3.1 %collective-permute-start.5 = (f32[1,512,512]{2,1,0:T(8,128)S(1)}, f32[1,512,512]{2,1,0:T(8,128)S(1)}, u32[]{:S(2)}, u32[]{:S(2)}) collective-permute-start(f32[1,512,512]{2,1,0:T(8,128)S(1)} %get-tuple-element.16), channel_id=1, source_target_pairs={{0,1},{1,2},{2,3},{3,4},{4,5},{5,6},{6,7},{7,8},{8,9},{9,10},{10,1... | collective-permute-start | bytes 3145736 | tf_op jit(solution)/shard_map/ppermute | solution.py:17
  101.1 0.1 collective-permute-done.4
  101.2 2.1 %collective-permute-done.5 = f32[1,512,512]{2,1,0:T(8,128)S(1)} collective-permute-done((f32[1,512,512]{2,1,0:T(8,128)S(1)}, f32[1,512,512]{2,1,0:T(8,128)S(1)}, u32[]{:S(2)}, u32[]{:S(2)}) %collective-permute-start.5) | collective-permute-done | bytes 1048608 | tf_op jit(solution)/shard_map/ppermute | solution.py:17
  103.3 4.5 %multiply_reduce_fusion = (f32[]{:T(128)}, f32[]{:T(128)}, f32[2,512,512]{2,1,0:T(8,128)}) fusion(f32[2,512,512]{2,1,0:T(8,128)S(1)} %fusion.25, f32[2,512,512]{2,1,0:T(8,128)S(1)} %copy-done.5, f32[]{:T(128)S(6)} %div.19, pred[2,512,512]{2,1,0:T(8,128)(4,1)S(1)} %get-tuple-element.13, f32[2,512,512]{2,1,0:T(8,128)S(1)} %copy-done, ...), kind=kLoop, calls=%fused_computation.44 | loop fusion | flops 8912894 | bytes 13107212 | tf_op jit(solution)/shard_map/reduce_sum | solution.py:83
  107.7 61.3 %all-reduce.3 = (f32[]{:T(128)}, f32[]{:T(128)}) all-reduce(f32[]{:T(128)} %get-tuple-element.3, f32[]{:T(128)} %get-tuple-element.2), channel_id=1, replica_groups=mesh['gz'=32] {'gz'}, use_global_device_ids=true, to_apply=%region_6.7 | all-reduce | flops 2 | bytes 16 | tf_op jit(solution)/shard_map/psum | solution.py:83
  173.6 6.9 %multiply_subtract_fusion = (f32[2,512,512]{2,1,0:T(8,128)}, f32[2,512,512]{2,1,0:T(8,128)}) fusion(f32[2,512,512]{2,1,0:T(8,128)} %get-tuple-element.10, f32[2,512,512]{2,1,0:T(8,128)} %get-tuple-element.11, f32[]{:T(128)S(6)} %div.21, f32[]{:T(128)S(6)} %div.23, f32[]{:T(128)S(6)} %div.19, pred[2,512,512]{2,1,0:T(8,128)(4,1)S(1)} %get-tuple-element.13, ...), kind=kLoop, calls=%fused_computation.42 | loop fusion | flops 6291456 | bytes 15204364 | tf_op jit(solution)/shard_map/sub | solution.py:94
  (16 shorter events, 0.0 us)
Async XLA Ops:
  0.6 5.9 %copy-start.6 = (s32[2,512,512]{2,1,0:T(8,128)S(1)}, s32[2,512,512]{2,1,0:T(8,128)}, u32[]{:S(2)}) copy-start(s32[2,512,512]{2,1,0:T(8,128)} %param.3) | copy-start | bytes 6291460
  2.9 5.4 %collective-permute-start = (s32[1,16,512]{2,1,0:T(8,128)S(1)}, s32[1,16,512]{2,1,0:T(8,128)S(1)}, u32[]{:S(2)}, u32[]{:S(2)}) collective-permute-start(s32[1,16,512]{2,1,0:T(8,128)S(1)} %get-tuple-element.21), channel_id=1, source_target_pairs={{0,1},{1,2},{2,3},{3,4},{4,5},{5,6},{6,7},{7,8},{8,9},{9,10},{10,1... | collective-permute-start | bytes 98312 | tf_op jit(solution)/shard_map/ppermute | solution.py:17
  5.3 5.2 %collective-permute-start.1 = (s32[1,16,512]{2,1,0:T(8,128)S(1)}, s32[1,16,512]{2,1,0:T(8,128)S(1)}, u32[]{:S(2)}, u32[]{:S(2)}) collective-permute-start(s32[1,16,512]{2,1,0:T(8,128)S(1)} %get-tuple-element.22), channel_id=1, source_target_pairs={{1,0},{2,1},{3,2},{4,3},{5,4},{6,5},{7,6},{8,7},{9,8},{10,9},{11,1... | collective-permute-start | bytes 98312 | tf_op jit(solution)/shard_map/ppermute | solution.py:19
  10.5 1.6 copy-start.8
  10.8 2.0 %copy-start = (f32[2,512,512]{2,1,0:T(8,128)S(1)}, f32[2,512,512]{2,1,0:T(8,128)}, u32[]{:S(2)}) copy-start(f32[2,512,512]{2,1,0:T(8,128)} %param.2) | copy-start | bytes 6291460
  10.8 2.6 %copy-start.7 = (s32[2,512,512]{2,1,0:T(8,128)S(1)}, s32[2,512,512]{2,1,0:T(8,128)}, u32[]{:S(2)}) copy-start(s32[2,512,512]{2,1,0:T(8,128)} %param.3) | copy-start | bytes 6291460
  15.7 8.9 %copy-start.1 = (f32[2,512,512]{2,1,0:T(8,128)}, f32[2,512,512]{2,1,0:T(8,128)S(1)}, u32[]{:S(2)}) copy-start(f32[2,512,512]{2,1,0:T(8,128)S(1)} %get-tuple-element.12) | copy-start | bytes 6291460
  15.7 8.9 %copy-start.3 = (f32[2,512,512]{2,1,0:T(8,128)}, f32[2,512,512]{2,1,0:T(8,128)S(1)}, u32[]{:S(2)}) copy-start(f32[2,512,512]{2,1,0:T(8,128)S(1)} %get-tuple-element.14) | copy-start | bytes 6291460
  15.9 6.7 %collective-permute-start.2 = (f32[1,512,512]{2,1,0:T(8,128)S(1)}, f32[1,512,512]{2,1,0:T(8,128)S(1)}, u32[]{:S(2)}, u32[]{:S(2)}) collective-permute-start(f32[1,512,512]{2,1,0:T(8,128)S(1)} %get-tuple-element.17), channel_id=1, source_target_pairs={{1,0},{2,1},{3,2},{4,3},{5,4},{6,5},{7,6},{8,7},{9,8},{10,9},{11,1... | collective-permute-start | bytes 3145736 | tf_op jit(solution)/shard_map/ppermute | solution.py:19
  17.2 7.4 %collective-permute-start.3 = (f32[1,512,512]{2,1,0:T(8,128)S(1)}, f32[1,512,512]{2,1,0:T(8,128)S(1)}, u32[]{:S(2)}, u32[]{:S(2)}) collective-permute-start(f32[1,512,512]{2,1,0:T(8,128)S(1)} %get-tuple-element.18), channel_id=1, source_target_pairs={{0,1},{1,2},{2,3},{3,4},{4,5},{5,6},{6,7},{7,8},{8,9},{9,10},{10,1... | collective-permute-start | bytes 3145736 | tf_op jit(solution)/shard_map/ppermute | solution.py:17
  96.2 7.1 %copy-start.2 = (f32[2,512,512]{2,1,0:T(8,128)}, f32[2,512,512]{2,1,0:T(8,128)S(1)}, u32[]{:S(2)}) copy-start(f32[2,512,512]{2,1,0:T(8,128)S(1)} %fusion.25) | copy-start | bytes 6291460
  96.2 7.1 %copy-start.4 = (f32[2,512,512]{2,1,0:T(8,128)S(1)}, f32[2,512,512]{2,1,0:T(8,128)}, u32[]{:S(2)}) copy-start(f32[2,512,512]{2,1,0:T(8,128)} %copy-done.3) | copy-start | bytes 6291460
  96.2 7.1 %copy-start.5 = (f32[2,512,512]{2,1,0:T(8,128)S(1)}, f32[2,512,512]{2,1,0:T(8,128)}, u32[]{:S(2)}) copy-start(f32[2,512,512]{2,1,0:T(8,128)} %get-tuple-element.11) | copy-start | bytes 6291460
  96.4 4.8 %collective-permute-start.4 = (f32[1,512,512]{2,1,0:T(8,128)S(1)}, f32[1,512,512]{2,1,0:T(8,128)S(1)}, u32[]{:S(2)}, u32[]{:S(2)}) collective-permute-start(f32[1,512,512]{2,1,0:T(8,128)S(1)} %get-tuple-element.15), channel_id=1, source_target_pairs={{1,0},{2,1},{3,2},{4,3},{5,4},{6,5},{7,6},{8,7},{9,8},{10,9},{11,1... | collective-permute-start | bytes 3145736 | tf_op jit(solution)/shard_map/ppermute | solution.py:19
  98.0 5.3 %collective-permute-start.5 = (f32[1,512,512]{2,1,0:T(8,128)S(1)}, f32[1,512,512]{2,1,0:T(8,128)S(1)}, u32[]{:S(2)}, u32[]{:S(2)}) collective-permute-start(f32[1,512,512]{2,1,0:T(8,128)S(1)} %get-tuple-element.16), channel_id=1, source_target_pairs={{0,1},{1,2},{2,3},{3,4},{4,5},{5,6},{6,7},{7,8},{8,9},{9,10},{10,1... | collective-permute-start | bytes 3145736 | tf_op jit(solution)/shard_map/ppermute | solution.py:17
where the time goes:
time: 181 us; the launch traced here: 180 us
  blocking collectives  124 us (69%)
  other arithmetic  24.9 us (14%)
  starting transfers between devices  14.9 us (8%)
  between operations  6.66 us (4%)
  waiting for transfers between devices  6.63 us (4%)
  local copies, waits for them, and re-layouts  3.1 us (2%)
    psum x2, blocking collectives, body(): lax.psum((jnp.sum(residual * precond), jnp.sum(applied * precond)), 'gz')  124 us
    ppermute x3, starting transfers between devices, extended_2(): lax.ppermute(tail, axis, [(i, (i + 1) % count) for i in range(ends)])  10.7 us
    reduce_sum x2, other arithmetic, body(): jnp.sum(applied * precond)  8.69 us
    sub x1, other arithmetic, body(): residual = residual - step_size * along  6.88 us
    div x2, other arithmetic, body(): precond = residual / diagonal  5.31 us
    ppermute x3, starting transfers between devices, extended_2(): lax.ppermute(head, axis, [((i + 1) % count, i) for i in range(ends)])  4.14 us
    ppermute x3, waiting for transfers between devices, extended_2(): lax.ppermute(tail, axis, [(i, (i + 1) % count) for i in range(ends)])  4.11 us
  transfers between devices with their start and end apart: 6, of which 5 were waited for; matrix products, arithmetic and copies ran while one was open for 1% of the time, Pallas kernels for 0%

commit v1 on v0

v1 whole, which is shorter than its diff:
```python
import functools
import math

import jax
import jax.numpy as jnp
from jax import lax
from jax.experimental import pallas as pl
from jax.experimental.pallas import tpu as pltpu
from jax.sharding import PartitionSpec as P

MESH = pl.DeviceIdType.MESH
TILE = 16
PAD = 8


def kernel(
    count, near, chunk,
    side_hbm, flag_hbm, sol_hbm, res_hbm,
    rhs, flags, r0, inv, solid, u0, u1, w0, w1, halo_r, halo_u, bits_out, bits_in,
    mine, near_got, far_got,
    in_sem, out_sem, bit_send, bit_recv, halo_send, halo_recv,
    near_send, near_recv, far_send, far_recv,
):
    depth, rows, cols = rhs.shape
    words = rows // 32
    chunks = rows // chunk
    tiles = chunk // TILE
    far = count // near
    me = lax.axis_index("gz")
    low, high = lax.rem(me, near), me // near
    first_side = 1 - lax.rem(me, 2)

    def load(plane, which):
        source, target = ((flag_hbm, flags), (side_hbm, rhs))[which]
        return pltpu.make_async_copy(source.at[plane], target.at[plane], in_sem.at[which, plane])

    for plane in range(depth):
        for which in range(2):
            load(plane, which).start()

    def present(side):
        return jnp.where(side == 0, me > 0, me < count - 1)

    def neighbour(side):
        return me - 1 + 2 * side

    near_ids = [high * near + lax.rem(low + j, near) for j in range(1, near)]
    far_ids = [lax.rem(high + j, far) * near + low for j in range(1, far)]
    barrier = pltpu.get_barrier_semaphore()
    for other in near_ids + far_ids:
        pl.semaphore_signal(barrier, inc=1, device_id=(other,), device_id_type=MESH)
    outside = (
        jnp.logical_and(low == 0, me > 0),
        jnp.logical_and(low == near - 1, me < count - 1),
    )
    for side in range(2):
        @pl.when(outside[side])
        def _():
            pl.semaphore_signal(barrier, inc=1, device_id=(neighbour(side),), device_id_type=MESH)

    blank = jnp.zeros((PAD, cols), jnp.float32)
    for ref in (u0, u1, solid):
        for plane in range(ref.shape[0]):
            ref[plane, 0:PAD, :] = blank
            ref[plane, rows + PAD:rows + 2 * PAD, :] = blank
    for side in range(2):
        @pl.when(jnp.logical_not(present(side)))
        def _():
            bits_in[side] = jnp.zeros((2, words, cols), jnp.int32)

            def clear(t, carry):
                at = pl.ds(pl.multiple_of(t * TILE, TILE), TILE)
                halo_r[side, at, :] = jnp.zeros((TILE, cols), jnp.float32)
                halo_u[side, at, :] = jnp.zeros((TILE, cols), jnp.float32)
                return carry

            lax.fori_loop(0, rows // TILE, clear, 0)

    outer = sorted({0, 1, depth - 2, depth - 1})
    for plane in range(depth):
        load(plane, 0).wait()

        def pack(j, word, plane=plane):
            at = pl.ds(pl.multiple_of(j * words, words), words)
            is_solid = flags[plane, at, :] == 2
            padded = pl.ds(pl.multiple_of(j * words + PAD, PAD), words)
            solid[plane + 2, padded, :] = jnp.where(is_solid, 1.0, 0.0)
            return word | jnp.left_shift(jnp.where(is_solid, 1, 0), j)

        word = lax.fori_loop(0, 32, pack, jnp.zeros((words, cols), jnp.int32))
        if plane in outer:
            bits_out[outer.index(plane)] = word

    peers = near + far - 2 + outside[0].astype(jnp.int32) + outside[1].astype(jnp.int32)
    pl.semaphore_wait(barrier, peers)

    def bit_copy(side):
        lead = 0 if side == 0 else len(outer) - 2
        return pltpu.make_async_remote_copy(
            src_ref=bits_out.at[pl.ds(lead, 2)],
            dst_ref=bits_in.at[1 - side],
            send_sem=bit_send.at[side],
            recv_sem=bit_recv.at[1 - side],
            device_id=(neighbour(side),),
            device_id_type=MESH,
        )

    for side in range(2):
        @pl.when(present(side))
        def _():
            bit_copy(side).start()

    def halo_copy(phase, side, k):
        at = pl.multiple_of(k * chunk, chunk)
        plane = side * (depth - 1)
        if phase == 0:
            source, target = r0.at[plane, pl.ds(at, chunk)], halo_r
        else:
            source, target = u1.at[plane, pl.ds(pl.multiple_of(at + PAD, PAD), chunk)], halo_u
        return pltpu.make_async_remote_copy(
            src_ref=source,
            dst_ref=target.at[1 - side, pl.ds(at, chunk)],
            send_sem=halo_send.at[phase, side, k],
            recv_sem=halo_recv.at[phase, 1 - side, k],
            device_id=(neighbour(side),),
            device_id_type=MESH,
        )

    def halo_arrival(phase, side, k):
        at = pl.multiple_of(k * chunk, chunk)
        target = halo_r if phase == 0 else halo_u
        return pltpu.make_async_remote_copy(
            src_ref=target.at[side, pl.ds(at, chunk)],
            dst_ref=target.at[side, pl.ds(at, chunk)],
            send_sem=halo_send.at[phase, side, k],
            recv_sem=halo_recv.at[phase, side, k],
            device_id=(neighbour(side),),
            device_id_type=MESH,
        )

    def send_halo(phase, side, k):
        @pl.when(present(side))
        def _():
            halo_copy(phase, side, k).start()

    def wait_halo(phase, side, k):
        @pl.when(present(side))
        def _():
            halo_arrival(phase, side, k).wait_recv()

    def row(k, t):
        return pl.multiple_of(k * chunk + t * TILE, TILE)

    for plane in range(depth):
        load(plane, 1).wait()
    edge_first = [0, depth - 1] + list(range(1, depth - 1))

    def mask_chunk(k, carry):
        for plane in edge_first:
            def mask_tile(t, carry, plane=plane):
                at = pl.ds(row(k, t), TILE)
                r0[plane, at, :] = jnp.where(flags[plane, at, :] == 1, rhs[plane, at, :], 0.0)
                return carry

            lax.fori_loop(0, tiles, mask_tile, 0)
        for side in range(2):
            send_halo(0, side, k)
        return carry

    lax.fori_loop(0, chunks, mask_chunk, 0)

    for side in range(2):
        @pl.when(present(side))
        def _():
            bit_copy(1 - side).wait_recv()
        for i in range(2):
            def unpack(j, carry, side=side, i=i):
                padded = pl.ds(pl.multiple_of(j * words + PAD, PAD), words)
                bit = jnp.bitwise_and(jnp.right_shift(bits_in[side, i], j), 1)
                solid[side * (depth + 2) + i, padded, :] = bit.astype(jnp.float32)
                return carry

            lax.fori_loop(0, 32, unpack, 0)

    column = lax.broadcasted_iota(jnp.int32, (TILE, cols), 1)

    def inplane(ref, plane, start):
        block = ref[plane, pl.ds(start, TILE + 2 * PAD), :]
        centre = block[PAD:PAD + TILE]
        total = block[PAD - 1:PAD - 1 + TILE] + block[PAD + 1:PAD + 1 + TILE]
        total = total + jnp.where(column == 0, 0.0, pltpu.roll(centre, 1, 1))
        total = total + jnp.where(column == cols - 1, 0.0, pltpu.roll(centre, cols - 1, 1))
        return centre, total

    def centre_of(ref, plane, start):
        return ref[plane, pl.ds(pl.multiple_of(start + PAD, PAD), TILE), :]

    def put(ref, plane, start, value):
        ref[plane, pl.ds(pl.multiple_of(start + PAD, PAD), TILE), :] = value

    def fold(value):
        total = value[0:8]
        for i in range(8, TILE, 8):
            total = total + value[i:i + 8]
        return total

    none = jnp.zeros((8, cols), jnp.float32)
    steps = rows // TILE

    def inverse(plane, start):
        _, total = inplane(solid, plane + 1, start)
        total = total + centre_of(solid, plane, start) + centre_of(solid, plane + 2, start)
        return 1.0 / jnp.maximum(6.0 - total, 1.0)

    def first(t, rz):
        start = pl.multiple_of(t * TILE, TILE)
        at = pl.ds(start, TILE)
        for plane in range(depth):
            value = jnp.where(flags[plane, at, :] == 1, inverse(plane + 1, start), 0.0)
            inv[plane + 1, at, :] = value
            residual = r0[plane, at, :]
            precond = residual * value
            put(u0, plane, start, precond)
            rz = rz + fold(residual * precond)
        for plane in (0, depth + 1):
            inv[plane, at, :] = inverse(plane, start)
        return rz

    rz = lax.fori_loop(0, steps, first, none)

    def local_part(field, scaled, out, plane, start):
        at = pl.ds(start, TILE)
        _, total = inplane(field, plane, start)
        if plane > 0:
            total = total + centre_of(field, plane - 1, start)
        if plane < depth - 1:
            total = total + centre_of(field, plane + 1, start)
        image = jnp.where(inv[plane + 1, at, :] > 0.0, scaled[plane, at, :] - total, 0.0)
        out[plane, at, :] = image
        return image

    def second(t, inner):
        start = pl.multiple_of(t * TILE, TILE)
        for plane in range(depth):
            image = local_part(u0, r0, w0, plane, start)
            if 0 < plane < depth - 1:
                put(u1, plane, start, image * inv[plane + 1, pl.ds(start, TILE), :])
                inner = inner + fold(image * centre_of(u0, plane, start))
        return inner

    inner = lax.fori_loop(0, steps, second, none)

    def edge_one(side, inner):
        plane = side * (depth - 1)

        def step(k, inner):
            wait_halo(0, side, k)

            def tile(t, inner):
                start = row(k, t)
                at = pl.ds(start, TILE)
                value = inv[plane + 1, at, :]
                beyond = halo_r[side, at, :] * inv[side * (depth + 1), at, :]
                image = jnp.where(value > 0.0, w0[plane, at, :] - beyond, 0.0)
                w0[plane, at, :] = image
                put(u1, plane, start, image * value)
                return inner + fold(image * centre_of(u0, plane, start))

            inner = lax.fori_loop(0, tiles, tile, inner)
            send_halo(1, side, k)
            return inner

        return lax.fori_loop(0, chunks, step, inner)

    inner = edge_one(first_side, inner)
    inner = edge_one(1 - first_side, inner)

    def lanes(value):
        total = value[:, 0:128]
        for i in range(128, cols, 128):
            total = total + value[:, i:i + 128]
        return total

    def near_copy(turn, j):
        return pltpu.make_async_remote_copy(
            src_ref=mine.at[turn, 0],
            dst_ref=near_got.at[turn, low],
            send_sem=near_send.at[turn, j],
            recv_sem=near_recv.at[turn, low],
            device_id=(near_ids[j - 1],),
            device_id_type=MESH,
        )

    def far_copy(turn, j):
        return pltpu.make_async_remote_copy(
            src_ref=mine.at[turn, 1],
            dst_ref=far_got.at[turn, high],
            send_sem=far_send.at[turn, j],
            recv_sem=far_recv.at[turn, high],
            device_id=(far_ids[j - 1],),
            device_id_type=MESH,
        )

    def sum_start(turn, one, two):
        mine[turn, 0, 0] = lanes(one)
        mine[turn, 0, 1] = lanes(two)
        for j in range(1, near):
            near_copy(turn, j).start()

    def arrived(turn, got, slot, send, recv, other):
        return pltpu.make_async_remote_copy(
            src_ref=got.at[turn, slot],
            dst_ref=got.at[turn, slot],
            send_sem=send.at[turn, 0],
            recv_sem=recv.at[turn, slot],
            device_id=(other,),
            device_id_type=MESH,
        )

    def sum_middle(turn):
        near_got[turn, low] = mine[turn, 0]
        for j in range(1, near):
            slot = lax.rem(low + j, near)
            arrived(turn, near_got, slot, near_send, near_recv, near_ids[j - 1]).wait_recv()
        total = near_got[turn, 0]
        for i in range(1, near):
            total = total + near_got[turn, i]
        mine[turn, 1] = total
        for j in range(1, far):
            far_copy(turn, j).start()

    def sum_end(turn):
        far_got[turn, high] = mine[turn, 1]
        for j in range(1, far):
            slot = lax.rem(high + j, far)
            arrived(turn, far_got, slot, far_send, far_recv, far_ids[j - 1]).wait_recv()
        total = far_got[turn, 0]
        for i in range(1, far):
            total = total + far_got[turn, i]
        return (
            jnp.sum(total[0], keepdims=True),
            jnp.sum(total[1], keepdims=True),
        )

    sum_start(0, rz, inner)

    def third(t, carry):
        start = pl.multiple_of(t * TILE, TILE)
        for plane in range(depth):
            local_part(u1, w0, w1, plane, start)
        return carry

    half = steps // 2
    lax.fori_loop(0, half, third, 0)
    sum_middle(0)
    lax.fori_loop(half, steps, third, 0)
    rz_old, product = sum_end(0)
    step_old = rz_old / product

    def contribution(plane, start, image, carry):
        at = pl.ds(start, TILE)
        along = w0[plane, at, :]
        residual = r0[plane, at, :] - step_old * along
        precond = centre_of(u0, plane, start) - step_old * centre_of(u1, plane, start)
        applied = along - step_old * image
        return (
            carry[0] + fold(residual * precond),
            carry[1] + fold(applied * precond),
        )

    carry = (none, none)
    for plane in range(1, depth - 1):
        def whole(t, carry, plane=plane):
            start = pl.multiple_of(t * TILE, TILE)
            return contribution(plane, start, w1[plane, pl.ds(start, TILE), :], carry)

        carry = lax.fori_loop(0, steps, whole, carry)

    def edge_two(side, carry):
        plane = side * (depth - 1)

        def step(k, carry):
            wait_halo(1, side, k)

            def tile(t, carry):
                start = row(k, t)
                at = pl.ds(start, TILE)
                image = w1[plane, at, :] - halo_u[side, at, :]
                image = jnp.where(inv[plane + 1, at, :] > 0.0, image, 0.0)
                w1[plane, at, :] = image
                return contribution(plane, start, image, carry)

            return lax.fori_loop(0, tiles, tile, carry)

        return lax.fori_loop(0, chunks, step, carry)

    carry = edge_two(first_side, carry)
    carry = edge_two(1 - first_side, carry)
    sum_start(1, *carry)
    sum_middle(1)
    rz_now, product = sum_end(1)
    blend = rz_now / rz_old
    step_size = rz_now / (product - blend * rz_now / step_old)

    def stores(plane, k):
        at = pl.ds(pl.multiple_of(k * chunk, chunk), chunk)
        return (
            pltpu.make_async_copy(rhs.at[plane, at], sol_hbm.at[plane, at], out_sem.at[0, plane, k]),
            pltpu.make_async_copy(w1.at[plane, at], res_hbm.at[plane, at], out_sem.at[1, plane, k]),
        )

    for plane in range(depth):
        def last(k, carry, plane=plane):
            def tile(t, carry):
                start = row(k, t)
                at = pl.ds(start, TILE)
                direction = centre_of(u0, plane, start)
                along = w0[plane, at, :]
                precond = direction - step_old * centre_of(u1, plane, start)
                applied = along - step_old * w1[plane, at, :]
                residual = r0[plane, at, :] - step_old * along
                rhs[plane, at, :] = step_old * direction + step_size * (precond + blend * direction)
                w1[plane, at, :] = residual - step_size * (applied + blend * along)
                return carry

            lax.fori_loop(0, tiles, tile, 0)
            for copy in stores(plane, k):
                copy.start()
            return carry

        lax.fori_loop(0, chunks, last, 0)

    for side in range(2):
        @pl.when(present(side))
        def _():
            bit_copy(side).wait_send()
            for phase in range(2):
                for k in range(chunks):
                    halo_copy(phase, side, k).wait_send()
    for turn in range(2):
        for j in range(1, near):
            near_copy(turn, j).wait_send()
        for j in range(1, far):
            far_copy(turn, j).wait_send()
    for plane in range(depth):
        for k in range(chunks):
            for copy in stores(plane, k):
                copy.wait()


def body(count, right_side, cell_flags):
    depth, rows, cols = right_side.shape
    near = math.gcd(count, 8)
    far = count // near
    chunk = math.gcd(rows, 64)
    chunks = rows // chunk
    f32 = jnp.float32
    field = pltpu.VMEM((depth, rows, cols), f32)
    padded = pltpu.VMEM((depth, rows + 2 * PAD, cols), f32)
    outer = len({0, 1, depth - 2, depth - 1})
    dma = pltpu.SemaphoreType.DMA
    shape = jax.ShapeDtypeStruct((depth, rows, cols), f32)
    return pl.pallas_call(
        functools.partial(kernel, count, near, chunk),
        out_shape=(shape, shape),
        in_specs=[pl.BlockSpec(memory_space=pl.ANY)] * 2,
        out_specs=(pl.BlockSpec(memory_space=pl.ANY),) * 2,
        scratch_shapes=[
            field,
            pltpu.VMEM((depth, rows, cols), jnp.int32),
            field,
            pltpu.VMEM((depth + 2, rows, cols), f32),
            pltpu.VMEM((depth + 4, rows + 2 * PAD, cols), f32),
            padded, padded, field, field,
            pltpu.VMEM((2, rows, cols), f32),
            pltpu.VMEM((2, rows, cols), f32),
            pltpu.VMEM((outer, rows // 32, cols), jnp.int32),
            pltpu.VMEM((2, 2, rows // 32, cols), jnp.int32),
            pltpu.VMEM((2, 2, 2, 8, 128), f32),
            pltpu.VMEM((2, near, 2, 8, 128), f32),
            pltpu.VMEM((2, far, 2, 8, 128), f32),
            dma((2, depth)),
            dma((2, depth, chunks)),
            dma((2,)), dma((2,)),
            dma((2, 2, chunks)), dma((2, 2, chunks)),
            dma((2, near)), dma((2, near)),
            dma((2, far)), dma((2, far)),
        ],
        compiler_params=pltpu.CompilerParams(
            collective_id=0, has_side_effects=True, vmem_limit_bytes=60 * 2**20
        ),
    )(right_side, cell_flags)


def solution(mesh):
    placed = (P("gz", None, None), P("gz", None, None))
    return jax.shard_map(
        functools.partial(body, mesh.shape["gz"]),
        mesh=mesh,
        in_specs=placed,
        out_specs=placed,
        check_vma=False,
    )
```

time: 181 us -> 75.4 us (0.42)
  blocking collectives: 124 us -> 0 us
  Pallas kernels: 0 us -> 70.1 us
  other arithmetic: 24.9 us -> 0 us
  starting transfers between devices: 14.9 us -> 0 us
  waiting for transfers between devices: 6.63 us -> 0 us
  between operations: 6.66 us -> 0.65 us
    psum x2 -> x0, blocking collectives: 124 us -> none  [body(): lax.psum((jnp.sum(residual * precond), jnp.sum(applied * precond)), 'gz')]
    pallas_call x0 -> x1, Pallas kernels: none -> 70.1 us  [body(): pl.pallas_call(functools.partial(kernel, count, near, chunk), out_shape=(...]
    ppermute x6 -> x0, starting transfers between devices: 14.9 us -> none  [the longest x3 10.7 us: extended_2(): lax.ppermute(tail, axis, [(i, (i + 1) % count) for i in range(ends)])]
    reduce_sum x3 -> x0, other arithmetic: 10.9 us -> none  [the longest x2 8.69 us: body(): jnp.sum(applied * precond)]
    sub x1 -> x0, other arithmetic: 6.88 us -> none  [body(): residual = residual - step_size * along]
    ppermute x6 -> x0, waiting for transfers between devices: 6.63 us -> none  [the longest x3 4.11 us: extended_2(): lax.ppermute(tail, axis, [(i, (i + 1) % count) for i in range(ends)])]
    div x2 -> x0, other arithmetic: 5.31 us -> none  [body(): precond = residual / diagonal]
    unnamed x18 -> x4, local copies, waits for them, and re-layouts: 2.49 us -> 4.55 us
  transfers between devices with their start and end apart: 6 -> 0, of which waited for: 5 -> 0; matrix products, arithmetic and copies ran while one was open for 1% -> 0% of each run, Pallas kernels for 0% -> 0%
where the time goes in v1:
time: 75.4 us; the launch traced here: 75.3 us
  Pallas kernels  70.1 us (93%)
  local copies, waits for them, and re-layouts  4.55 us (6%)
    pallas_call x1, Pallas kernels, body(): pl.pallas_call(functools.partial(kernel, count, near, chunk), out_shape=(...  70.1 us
    unnamed x4, local copies, waits for them, and re-layouts  4.55 us

profile of v1, /device:TPU:0, one launch (start us, length us, event | category | flops | bytes accessed | tf_op | source)
XLA Modules:
  0.0 75.3 jit_solution(11699758088844758797)
XLA Ops:
  0.6 70.1 %shard_map.41 = (f32[2,512,512]{2,1,0:T(8,128)}, f32[2,512,512]{2,1,0:T(8,128)}) custom-call(f32[2,512,512]{2,1,0:T(8,128)} %side_hbm.1, s32[2,512,512]{2,1,0:T(8,128)} %flag_hbm.1), custom_call_target="tpu_custom_call" | custom-call | tf_op jit(solution)/shard_map/pallas_call | solution.py:463
  70.7 0.0 copy-start
  70.7 3.2 %copy.6 = f32[2,512,512]{2,1,0:T(8,128)} copy(f32[2,512,512]{2,1,0:T(8,128)} %get-tuple-element.4) | data formatting | bytes 4194304
  73.9 0.0 copy-done
  73.9 1.3 %copy.7 = f32[2,512,512]{2,1,0:T(8,128)} copy(f32[2,512,512]{2,1,0:T(8,128)S(1)} %copy-done) | data formatting | bytes 4194304
Async XLA Ops:
  70.7 3.2 %copy-start = (f32[2,512,512]{2,1,0:T(8,128)S(1)}, f32[2,512,512]{2,1,0:T(8,128)}, u32[]{:S(2)}) copy-start(f32[2,512,512]{2,1,0:T(8,128)} %get-tuple-element.5) | copy-start | bytes 6291460

commit v2 on v1

--- a/solution.py
+++ b/solution.py
@@ -11,14 +11,16 @@
 MESH = pl.DeviceIdType.MESH
 TILE = 16
 PAD = 8
+AHEAD = 2
+VMEM_BYTES = 67_043_328
 
 
 def kernel(
     count, near, chunk,
-    side_hbm, flag_hbm, sol_hbm, res_hbm,
+    side_hbm, flag_hbm, sol_ref, res_ref,
     rhs, flags, r0, inv, solid, u0, u1, w0, w1, halo_r, halo_u, bits_out, bits_in,
     mine, near_got, far_got,
-    in_sem, out_sem, bit_send, bit_recv, halo_send, halo_recv,
+    in_sem, bit_send, bit_recv, halo_send, halo_recv,
     near_send, near_recv, far_send, far_recv,
 ):
     depth, rows, cols = rhs.shape
@@ -75,40 +77,6 @@
                 return carry
 
             lax.fori_loop(0, rows // TILE, clear, 0)
-
-    outer = sorted({0, 1, depth - 2, depth - 1})
-    for plane in range(depth):
-        load(plane, 0).wait()
-
-        def pack(j, word, plane=plane):
-            at = pl.ds(pl.multiple_of(j * words, words), words)
-            is_solid = flags[plane, at, :] == 2
-            padded = pl.ds(pl.multiple_of(j * words + PAD, PAD), words)
-            solid[plane + 2, padded, :] = jnp.where(is_solid, 1.0, 0.0)
-            return word | jnp.left_shift(jnp.where(is_solid, 1, 0), j)
-
-        word = lax.fori_loop(0, 32, pack, jnp.zeros((words, cols), jnp.int32))
-        if plane in outer:
-            bits_out[outer.index(plane)] = word
-
-    peers = near + far - 2 + outside[0].astype(jnp.int32) + outside[1].astype(jnp.int32)
-    pl.semaphore_wait(barrier, peers)
-
-    def bit_copy(side):
-        lead = 0 if side == 0 else len(outer) - 2
-        return pltpu.make_async_remote_copy(
-            src_ref=bits_out.at[pl.ds(lead, 2)],
-            dst_ref=bits_in.at[1 - side],
-            send_sem=bit_send.at[side],
-            recv_sem=bit_recv.at[1 - side],
-            device_id=(neighbour(side),),
-            device_id_type=MESH,
-        )
-
-    for side in range(2):
-        @pl.when(present(side))
-        def _():
-            bit_copy(side).start()
 
     def halo_copy(phase, side, k):
         at = pl.multiple_of(k * chunk, chunk)
@@ -152,10 +120,11 @@
         return pl.multiple_of(k * chunk + t * TILE, TILE)
 
     for plane in range(depth):
+        load(plane, 0).wait()
         load(plane, 1).wait()
     edge_first = [0, depth - 1] + list(range(1, depth - 1))
 
-    def mask_chunk(k, carry):
+    def mask_rows(k):
         for plane in edge_first:
             def mask_tile(t, carry, plane=plane):
                 at = pl.ds(row(k, t), TILE)
@@ -163,11 +132,53 @@
                 return carry
 
             lax.fori_loop(0, tiles, mask_tile, 0)
+
+    def send_both(phase, k):
         for side in range(2):
-            send_halo(0, side, k)
+            send_halo(phase, side, k)
+
+    def mask_chunk(k, carry):
+        mask_rows(k)
+        send_both(0, k)
         return carry
 
-    lax.fori_loop(0, chunks, mask_chunk, 0)
+    mask_rows(0)
+    peers = near + far - 2 + outside[0].astype(jnp.int32) + outside[1].astype(jnp.int32)
+    pl.semaphore_wait(barrier, peers)
+
+    send_both(0, 0)
+
+    outer = sorted({0, 1, depth - 2, depth - 1})
+    for plane in range(depth):
+
+        def pack(j, word, plane=plane):
+            at = pl.ds(pl.multiple_of(j * words, words), words)
+            is_solid = flags[plane, at, :] == 2
+            padded = pl.ds(pl.multiple_of(j * words + PAD, PAD), words)
+            solid[plane + 2, padded, :] = jnp.where(is_solid, 1.0, 0.0)
+            return word | jnp.left_shift(jnp.where(is_solid, 1, 0), j)
+
+        word = lax.fori_loop(0, 32, pack, jnp.zeros((words, cols), jnp.int32))
+        if plane in outer:
+            bits_out[outer.index(plane)] = word
+
+    def bit_copy(side):
+        lead = 0 if side == 0 else len(outer) - 2
+        return pltpu.make_async_remote_copy(
+            src_ref=bits_out.at[pl.ds(lead, 2)],
+            dst_ref=bits_in.at[1 - side],
+            send_sem=bit_send.at[side],
+            recv_sem=bit_recv.at[1 - side],
+            device_id=(neighbour(side),),
+            device_id_type=MESH,
+        )
+
+    for side in range(2):
+        @pl.when(present(side))
+        def _():
+            bit_copy(side).start()
+
+    lax.fori_loop(1, chunks, mask_chunk, 0)
 
     for side in range(2):
         @pl.when(present(side))
@@ -250,7 +261,7 @@
 
     inner = lax.fori_loop(0, steps, second, none)
 
-    def edge_one(side, inner):
+    def edge_one(side, inner, ahead):
         plane = side * (depth - 1)
 
         def step(k, inner):
@@ -267,13 +278,17 @@
                 return inner + fold(image * centre_of(u0, plane, start))
 
             inner = lax.fori_loop(0, tiles, tile, inner)
-            send_halo(1, side, k)
+
+            @pl.when(k < ahead)
+            def _():
+                send_halo(1, side, k)
+
             return inner
 
         return lax.fori_loop(0, chunks, step, inner)
 
-    inner = edge_one(first_side, inner)
-    inner = edge_one(1 - first_side, inner)
+    inner = edge_one(first_side, inner, chunks)
+    inner = edge_one(1 - first_side, inner, AHEAD)
 
     def lanes(value):
         total = value[:, 0:128]
@@ -344,6 +359,12 @@
 
     sum_start(0, rz, inner)
 
+    def send_rest(k, carry):
+        send_halo(1, 1 - first_side, k)
+        return carry
+
+    lax.fori_loop(AHEAD, chunks, send_rest, 0)
+
     def third(t, carry):
         start = pl.multiple_of(t * TILE, TILE)
         for plane in range(depth):
@@ -402,33 +423,20 @@
     blend = rz_now / rz_old
     step_size = rz_now / (product - blend * rz_now / step_old)
 
-    def stores(plane, k):
-        at = pl.ds(pl.multiple_of(k * chunk, chunk), chunk)
-        return (
-            pltpu.make_async_copy(rhs.at[plane, at], sol_hbm.at[plane, at], out_sem.at[0, plane, k]),
-            pltpu.make_async_copy(w1.at[plane, at], res_hbm.at[plane, at], out_sem.at[1, plane, k]),
-        )
-
     for plane in range(depth):
-        def last(k, carry, plane=plane):
-            def tile(t, carry):
-                start = row(k, t)
-                at = pl.ds(start, TILE)
-                direction = centre_of(u0, plane, start)
-                along = w0[plane, at, :]
-                precond = direction - step_old * centre_of(u1, plane, start)
-                applied = along - step_old * w1[plane, at, :]
-                residual = r0[plane, at, :] - step_old * along
-                rhs[plane, at, :] = step_old * direction + step_size * (precond + blend * direction)
-                w1[plane, at, :] = residual - step_size * (applied + blend * along)
-                return carry
-
-            lax.fori_loop(0, tiles, tile, 0)
-            for copy in stores(plane, k):
-                copy.start()
+        def last(t, carry, plane=plane):
+            start = pl.multiple_of(t * TILE, TILE)
+            at = pl.ds(start, TILE)
+            direction = centre_of(u0, plane, start)
+            along = w0[plane, at, :]
+            precond = direction - step_old * centre_of(u1, plane, start)
+            applied = along - step_old * w1[plane, at, :]
+            residual = r0[plane, at, :] - step_old * along
+            sol_ref[plane, at, :] = step_old * direction + step_size * (precond + blend * direction)
+            res_ref[plane, at, :] = residual - step_size * (applied + blend * along)
             return carry
 
-        lax.fori_loop(0, chunks, last, 0)
+        lax.fori_loop(0, steps, last, 0)
 
     for side in range(2):
         @pl.when(present(side))
@@ -442,10 +450,6 @@
             near_copy(turn, j).wait_send()
         for j in range(1, far):
             far_copy(turn, j).wait_send()
-    for plane in range(depth):
-        for k in range(chunks):
-            for copy in stores(plane, k):
-                copy.wait()
 
 
 def body(count, right_side, cell_flags):
@@ -459,12 +463,12 @@
     padded = pltpu.VMEM((depth, rows + 2 * PAD, cols), f32)
     outer = len({0, 1, depth - 2, depth - 1})
     dma = pltpu.SemaphoreType.DMA
-    shape = jax.ShapeDtypeStruct((depth, rows, cols), f32)
+    grant = VMEM_BYTES - 8 * right_side.size - 2**19
     return pl.pallas_call(
         functools.partial(kernel, count, near, chunk),
-        out_shape=(shape, shape),
-        in_specs=[pl.BlockSpec(memory_space=pl.ANY)] * 2,
-        out_specs=(pl.BlockSpec(memory_space=pl.ANY),) * 2,
+        out_shape=(field, field),
+        in_specs=[pl.BlockSpec(memory_space=pltpu.HBM)] * 2,
+        out_specs=(pl.BlockSpec(memory_space=pltpu.VMEM),) * 2,
         scratch_shapes=[
             field,
             pltpu.VMEM((depth, rows, cols), jnp.int32),
@@ -480,14 +484,13 @@
             pltpu.VMEM((2, near, 2, 8, 128), f32),
             pltpu.VMEM((2, far, 2, 8, 128), f32),
             dma((2, depth)),
-            dma((2, depth, chunks)),
             dma((2,)), dma((2,)),
             dma((2, 2, chunks)), dma((2, 2, chunks)),
             dma((2, near)), dma((2, near)),
             dma((2, far)), dma((2, far)),
         ],
         compiler_params=pltpu.CompilerParams(
-            collective_id=0, has_side_effects=True, vmem_limit_bytes=60 * 2**20
+            collective_id=0, has_side_effects=True, vmem_limit_bytes=grant
         ),
     )(right_side, cell_flags)
 

time: 75.4 us -> 67.5 us (0.90)
  Pallas kernels: 70.1 us -> 64.1 us
  local copies, waits for them, and re-layouts: 4.55 us -> 2.64 us
    pallas_call x1, Pallas kernels: 70.1 us -> 64.1 us  [body(): pl.pallas_call(functools.partial(kernel, count, near, chunk), out_shape=(...]
    unnamed x4 -> x2, local copies, waits for them, and re-layouts: 4.55 us -> 2.64 us
where the time goes in v2:
time: 67.5 us; the launch traced here: 67.4 us
  Pallas kernels  64.1 us (95%)
  local copies, waits for them, and re-layouts  2.64 us (4%)
    pallas_call x1, Pallas kernels, body(): pl.pallas_call(functools.partial(kernel, count, near, chunk), out_shape=(...  64.1 us
    unnamed x2, local copies, waits for them, and re-layouts  2.64 us

profile of v2, /device:TPU:0, one launch (start us, length us, event | category | flops | bytes accessed | tf_op | source)
XLA Modules:
  0.0 67.4 jit_solution(11676842012484414083)
XLA Ops:
  0.6 64.1 %shard_map.41 = (f32[2,512,512]{2,1,0:T(8,128)S(1)}, f32[2,512,512]{2,1,0:T(8,128)S(1)}) custom-call(f32[2,512,512]{2,1,0:T(8,128)} %side_hbm.1, s32[2,512,512]{2,1,0:T(8,128)} %flag_hbm.1), custom_call_target="tpu_custom_call" | custom-call | tf_op jit(solution)/shard_map/pallas_call | solution.py:467
  64.7 1.3 %copy.6 = f32[2,512,512]{2,1,0:T(8,128)} copy(f32[2,512,512]{2,1,0:T(8,128)S(1)} %get-tuple-element.2) | data formatting | bytes 4194304
  66.0 1.3 %copy.7 = f32[2,512,512]{2,1,0:T(8,128)} copy(f32[2,512,512]{2,1,0:T(8,128)S(1)} %get-tuple-element.3) | data formatting | bytes 4194304
